TPU v7x, 32 devices: a whole 2x2x4 slice. The times are simulated.
32 devices in a mesh: layer: 4 (over z), row: 2 (over core), col: 4 (over y, x).
Axes of the slice: x: 2, y: 2, z: 4, core: 2. Of those that a mesh axis runs over, the one named last changes fastest.
Arguments:
- panels: float32 [4096, 8192], P('row', ('layer', 'col')), may hold values from -0.0625 to 0.0625
- eigvecs: float32 [8192, 2048], P(('layer', 'row'), 'col'), may hold values from -6 to 6
Outputs:
- result: float32 [4096, 2048], P('row', 'col')
All inputs are finite; a program needn't handle non-finite values.
Results may differ from a plain program's by a relative error of at most 0.0001.
Values sent between devices are 32-bit elements; how exact they have to be, the bound alone decides.
No kernel may reach another device: no remote copies, remote signals or barrier semaphores. Data moves between devices by JAX's collectives and lax.ppermute only.
A program may use at most 64 MiB of HBM per device.

v0:
```python
import jax
import jax.numpy as jnp
from jax import lax
from jax.sharding import PartitionSpec as P


def local(panels, eigvecs):
    layer_vecs = lax.all_gather(eigvecs, "row", axis=0, tiled=True)
    partial_sum = jnp.dot(
        lax.all_gather(panels, "col", axis=1, tiled=True),
        layer_vecs,
        preferred_element_type=jnp.float32,
        precision=lax.Precision.HIGHEST,
    )
    result = lax.psum(partial_sum, "layer")
    return result


def solution(mesh):
    in_specs = (P("row", ("layer", "col")), P(("layer", "row"), "col"))
    out_specs = P("row", "col")
    return jax.shard_map(local, mesh=mesh, in_specs=in_specs, out_specs=out_specs, check_vma=False)
```

profile of v0, /device:TPU:0, one launch (start us, length us, event | category | flops | bytes accessed | tf_op | source)
XLA Modules:
  0.0 383.9 jit_solution(4425001586556484213)
XLA Ops:
  6.5 0.0 all-gather.5.cloned.1.call-start
  6.5 0.7 all-gather.5.cloned.1.call-update
  7.3 0.0 all-gather.3.cloned.1.call-start
  7.3 0.7 all-gather.3.cloned.1.call-update
  8.0 0.0 all-reduce.2.cloned.1.call-start
  8.1 17.2 %all-gather.5.cloned.1.call-done = f32[2048,512]{1,0:T(8,128)} async-done(((f32[1024,512]{1,0:T(8,128)}), f32[2048,512]{1,0:T(8,128)}) %all-gather.5.cloned.1.call-update) | async-done | bytes 4194320 | tf_op jit(solution)/shard_map/all_gather | solution.py:8
  25.3 160.3 %all-gather.3.cloned.1.call-done = f32[2048,2048]{1,0:T(8,128)} async-done(((f32[2048,512]{1,0:T(8,128)}), f32[2048,2048]{1,0:T(8,128)}) %all-gather.3.cloned.1.call-update) | async-done | bytes 16777232 | tf_op jit(solution)/shard_map/all_gather | solution.py:10
  185.6 31.9 %fusion = f32[2048,512]{1,0:T(8,128)} fusion(f32[2048,2048]{1,0:T(8,128)} %all-gather.3.cloned.1.call-done, f32[2048,512]{1,0:T(8,128)} %all-gather.5.cloned.1.call-done), kind=kOutput, calls=%fused_computation | convolution fusion | flops 25769803776 | bytes 25165824 | tf_op jit(solution)/shard_map/dot_general | solution.py:9
  217.6 0.0 all-reduce.2.cloned.1.call-update
  217.6 155.1 %all-reduce.2.cloned.1.call-done = f32[2048,512]{1,0:T(8,128)} async-done(((f32[2048,512]{1,0:T(8,128)}), f32[2048,512]{1,0:T(8,128)}) %all-reduce.2.cloned.1.call-update) | async-done | bytes 4194320 | tf_op jit(solution)/shard_map/psum | solution.py:15
  372.7 4.6 %copy.4 = f32[2048,512]{1,0:T(8,128)} copy(f32[2048,512]{1,0:T(8,128)} %all-reduce.2.cloned.1.call-done) | data formatting | bytes 8388608
Async XLA Ops:
  6.5 18.8 %all-gather.5.cloned.1.call-start = ((), (), s32[]{:S(2)}) async-start(), calls=%async_computation.1 | async-start | bytes 6291456 | tf_op jit(solution)/shard_map/all_gather | solution.py:8
  7.3 178.4 %all-gather.3.cloned.1.call-start = ((), (), s32[]{:S(2)}) async-start(), calls=%async_computation | async-start | bytes 20971520 | tf_op jit(solution)/shard_map/all_gather | solution.py:10
  8.0 364.7 %all-reduce.2.cloned.1.call-start = ((), (), s32[]{:S(2)}) async-start(), calls=%async_computation.2 | async-start | bytes 8388608 | tf_op jit(solution)/shard_map/psum | solution.py:15
Sparse Core Ops, SparseCore 0:
  8.9 16.3 all-gather.4
  27.1 158.4 all-gather.2
  217.7 154.9 all-reduce.1
where the time goes:
time: 384 us
  waiting for transfers between devices  334 us (87%)
  matrix products  31.9 us (8%)
  between operations  13.1 us (3%)
  local copies, waits for them, and re-layouts  4.64 us (1%)
    all_gather x1, waiting for transfers between devices, local(): lax.all_gather(panels, 'col', axis=1, tiled=True)  160 us
    psum x1, waiting for transfers between devices, local(): result = lax.psum(partial_sum, 'layer')  155 us
    dot_general x1, matrix products, local(): jnp.dot(lax.all_gather(panels, 'col', axis=1, tiled=True), layer_vecs, pr...  31.9 us
    all_gather x1, waiting for transfers between devices, local(): layer_vecs = lax.all_gather(eigvecs, 'row', axis=0, tiled=True)  17.2 us
  transfers between devices with their start and end apart: 3, of which 3 were waited for; matrix products, arithmetic and copies ran while one was open for 0% of the time, Pallas kernels for 0%

commit v1 on v0

--- a/solution.py
+++ b/solution.py
@@ -2,6 +2,15 @@
 import jax.numpy as jnp
 from jax import lax
 from jax.sharding import PartitionSpec as P
+
+
+def add_in_pairs(array, axis):
+    size = lax.axis_size(axis)
+    acc, stride = (array, 1)
+    while stride < size:
+        acc = acc + lax.ppermute(acc, axis, [(i, i ^ stride) for i in range(size)])
+        stride = 2 * stride
+    return acc
 
 
 def local(panels, eigvecs):
@@ -12,7 +21,7 @@
         preferred_element_type=jnp.float32,
         precision=lax.Precision.HIGHEST,
     )
-    result = lax.psum(partial_sum, "layer")
+    result = add_in_pairs(partial_sum, "layer")
     return result
 
 

time: 384 us -> 503 us (1.31)
  waiting for transfers between devices: 334 us -> 449 us
    ppermute x0 -> x2, waiting for transfers between devices: none -> 270 us  [add_in_pairs(): acc = acc + lax.ppermute(acc, axis, [(i, i ^ stride) for i in range(size)])]
    psum x1 -> x0, waiting for transfers between devices: 155 us -> none  [local(): result = lax.psum(partial_sum, 'layer')]
  transfers between devices with their start and end apart: 3 -> 4, of which waited for: 3 -> 4; matrix products, arithmetic and copies ran while one was open for 0% -> 0% of each run, Pallas kernels for 0% -> 0%
where the time goes in v1:
time: 503 us
  waiting for transfers between devices  449 us (89%)
  matrix products  32 us (6%)
  between operations  13.4 us (3%)
    ppermute x2, waiting for transfers between devices, add_in_pairs(): acc = acc + lax.ppermute(acc, axis, [(i, i ^ stride) for i in range(size)])  270 us
    all_gather x1, waiting for transfers between devices, local(): lax.all_gather(panels, 'col', axis=1, tiled=True)  160 us
    dot_general x1, matrix products, local(): jnp.dot(lax.all_gather(panels, 'col', axis=1, tiled=True), layer_vecs, pr...  32 us
    all_gather x1, waiting for transfers between devices, local(): layer_vecs = lax.all_gather(eigvecs, 'row', axis=0, tiled=True)  17.3 us
  transfers between devices with their start and end apart: 4, of which 4 were waited for; matrix products, arithmetic and copies ran while one was open for 0% of the time, Pallas kernels for 0%

profile of v1, /device:TPU:0, one launch (start us, length us, event | category | flops | bytes accessed | tf_op | source)
XLA Modules:
  0.0 502.9 jit_solution(4564204904647918365)
XLA Ops:
  6.5 0.0 all-gather.5.cloned.1.call-start
  6.5 0.7 all-gather.5.cloned.1.call-update
  7.3 0.0 all-gather.3.cloned.1.call-start
  7.3 0.7 all-gather.3.cloned.1.call-update
  8.0 17.3 %all-gather.5.cloned.1.call-done = f32[2048,512]{1,0:T(8,128)} async-done(((f32[1024,512]{1,0:T(8,128)}), f32[2048,512]{1,0:T(8,128)}) %all-gather.5.cloned.1.call-update) | async-done | bytes 4194320 | tf_op jit(solution)/shard_map/all_gather | solution.py:17
  25.3 160.3 %all-gather.3.cloned.1.call-done = f32[2048,2048]{1,0:T(8,128)} async-done(((f32[2048,512]{1,0:T(8,128)}), f32[2048,2048]{1,0:T(8,128)}) %all-gather.3.cloned.1.call-update) | async-done | bytes 16777232 | tf_op jit(solution)/shard_map/all_gather | solution.py:19
  185.6 32.0 %fusion = f32[2048,512]{1,0:T(8,128)S(1)} fusion(f32[2048,2048]{1,0:T(8,128)} %all-gather.3.cloned.1.call-done, f32[2048,512]{1,0:T(8,128)} %all-gather.5.cloned.1.call-done), kind=kOutput, calls=%fused_computation | convolution fusion | flops 25769803776 | bytes 25165824 | tf_op jit(solution)/shard_map/dot_general | solution.py:18
  217.6 1.6 collective-permute-start
  219.2 90.7 %collective-permute-done = f32[2048,512]{1,0:T(8,128)S(1)} collective-permute-done((f32[2048,512]{1,0:T(8,128)S(1)}, f32[2048,512]{1,0:T(8,128)S(1)}, u32[]{:S(2)}, u32[]{:S(2)}) %collective-permute-start) | collective-permute-done | bytes 4194336 | tf_op jit(solution)/shard_map/ppermute | solution.py:11
  309.9 1.0 add.6
  310.9 2.5 collective-permute-start.1
  313.3 179.7 %collective-permute-done.1 = f32[2048,512]{1,0:T(8,128)S(1)} collective-permute-done((f32[2048,512]{1,0:T(8,128)S(1)}, f32[2048,512]{1,0:T(8,128)S(1)}, u32[]{:S(2)}, u32[]{:S(2)}) %collective-permute-start.1) | collective-permute-done | bytes 4194336 | tf_op jit(solution)/shard_map/ppermute | solution.py:11
  493.0 3.0 add.7
Async XLA Ops:
  6.5 18.8 %all-gather.5.cloned.1.call-start = ((), (), s32[]{:S(2)}) async-start(), calls=%async_computation.1 | async-start | bytes 6291456 | tf_op jit(solution)/shard_map/all_gather | solution.py:17
  7.3 178.4 %all-gather.3.cloned.1.call-start = ((), (), s32[]{:S(2)}) async-start(), calls=%async_computation | async-start | bytes 20971520 | tf_op jit(solution)/shard_map/all_gather | solution.py:19
  217.6 92.2 %collective-permute-start = (f32[2048,512]{1,0:T(8,128)S(1)}, f32[2048,512]{1,0:T(8,128)S(1)}, u32[]{:S(2)}, u32[]{:S(2)}) collective-permute-start(f32[2048,512]{1,0:T(8,128)S(1)} %fusion), channel_id=1, source_target_pairs={{0,8},{8,0},{16,24},{24,16},{1,9},{9,1},{17,25},{25,17},{2,10},{10... | collective-permute-start | bytes 12582920 | tf_op jit(solution)/shard_map/ppermute | solution.py:11
  310.9 182.1 %collective-permute-start.1 = (f32[2048,512]{1,0:T(8,128)S(1)}, f32[2048,512]{1,0:T(8,128)S(1)}, u32[]{:S(2)}, u32[]{:S(2)}) collective-permute-start(f32[2048,512]{1,0:T(8,128)S(1)} %add.6), channel_id=1, source_target_pairs={{0,16},{8,24},{16,0},{24,8},{1,17},{9,25},{17,1},{25,9},{2,18},{10... | collective-permute-start | bytes 12582920 | tf_op jit(solution)/shard_map/ppermute | solution.py:11
Sparse Core Ops, SparseCore 0:
  8.9 16.3 all-gather.4
  27.1 158.4 all-gather.2
